TPU v7x, 32 devices: a whole 2x2x4 slice. The times are simulated.
32 devices in a mesh: dp: 8 (over z, x), mp: 4 (over y, core).
Axes of the slice: x: 2, y: 2, z: 4, core: 2. Of those that a mesh axis runs over, the one named last changes fastest.
Arguments:
- state_end: float32 [2048, 512], P('dp', 'mp'), may hold values from -6 to 6
- adjoint_end: float32 [2048, 512], P('dp', 'mp'), may hold values from -6 to 6
- increments: bfloat16 [8, 2048, 512], P(None, 'dp'), may hold values from -1.5 to 1.5
- w_in: bfloat16 [512, 2048], P(None, 'mp'), may hold values from -0.25 to 0.25
- b_in: float32 [2048], P('mp'), may hold values from -3 to 3
- w_out: bfloat16 [2048, 512], P('mp'), may hold values from -0.125 to 0.125
- b_out: float32 [512], replicated, may hold values from -3 to 3
- sigma: float32 [512], replicated, may hold values from 0.1 to 1
Outputs:
- state_start: float32 [2048, 512], P('dp', 'mp')
- adjoint_start: float32 [2048, 512], P('dp', 'mp')
- grad_w_in: float32 [512, 2048], P('dp', 'mp')
- grad_w_out: float32 [2048, 512], P('mp', 'dp')
All inputs are finite; a program needn't handle non-finite values.
Results may differ from a plain program's by a relative error of at most 0.005.
Values may be sent and summed in bfloat16 or wider, within the bound.
A program may use at most 64 MiB of HBM per device.

v0:
```python
import jax
import jax.numpy as jnp
from jax import lax
from jax.sharding import PartitionSpec as P

STEPS = 8


def local_terms(z_low, a_low, w_in, b_in, w_out):
    hidden = jnp.tanh(jnp.dot(z_low, w_in, preferred_element_type=jnp.float32) + b_in)
    hidden_low = hidden.astype(jnp.bfloat16)
    drift_part = jnp.dot(hidden_low, w_out, preferred_element_type=jnp.float32)
    back = jnp.dot(a_low, w_out.T, preferred_element_type=jnp.float32)
    delta = (back * (1.0 - hidden * hidden)).astype(jnp.bfloat16)
    pull_part = jnp.dot(delta, w_in.T, preferred_element_type=jnp.float32)
    grad_in = jnp.dot(z_low.T, delta, preferred_element_type=jnp.float32)
    grad_out = jnp.dot(hidden_low.T, a_low, preferred_element_type=jnp.float32)
    return (drift_part, pull_part, grad_in, grad_out)


def body(state_end, adjoint_end, increments, w_in, b_in, w_out, b_out, sigma):
    step_size = 1.0 / STEPS
    share_rows = state_end.shape[0] // lax.axis_size("mp")
    row_start = lax.axis_index("mp") * share_rows
    state_rows, adjoint_rows = (
        lax.all_to_all(state_end, "mp", split_axis=0, concat_axis=1, tiled=True),
        lax.all_to_all(adjoint_end, "mp", split_axis=0, concat_axis=1, tiled=True),
    )
    w_in_whole, w_out_whole, b_in_whole = (
        lax.all_gather(w_in, "mp", axis=1, tiled=True),
        lax.all_gather(w_out, "mp", axis=0, tiled=True),
        lax.all_gather(b_in.astype(jnp.bfloat16), "mp", axis=0, tiled=True).astype(b_in.dtype),
    )
    noise_rows = lax.dynamic_slice_in_dim(increments, row_start, share_rows, 1)
    full_zero = (
        jnp.zeros((w_in_whole.shape[0], w_in_whole.shape[1]), jnp.float32),
        jnp.zeros((w_out_whole.shape[0], w_out_whole.shape[1]), jnp.float32),
    )

    def advance(counter, carry):
        state, adjoint, acc_in, acc_out = carry
        level = STEPS - 1 - counter
        noise_now = lax.dynamic_index_in_dim(noise_rows, level, 0, keepdims=False).astype(
            jnp.float32
        )
        drift_sum, pull_sum, grad_in, grad_out = local_terms(
            state.astype(jnp.bfloat16),
            adjoint.astype(jnp.bfloat16),
            w_in_whole,
            b_in_whole,
            w_out_whole,
        )
        adjoint = adjoint + step_size * pull_sum
        state = state - step_size * (drift_sum + b_out) - sigma * noise_now
        return (state, adjoint, acc_in + grad_in, acc_out + grad_out)

    state_done, adjoint_done, full_in, full_out = lax.fori_loop(
        0, STEPS, advance, (state_rows, adjoint_rows) + full_zero
    )
    acc_in, acc_out = (
        lax.psum_scatter(full_in, "mp", scatter_dimension=1, tiled=True),
        lax.psum_scatter(full_out, "mp", scatter_dimension=0, tiled=True),
    )
    state, adjoint = (
        lax.all_to_all(state_done, "mp", split_axis=1, concat_axis=0, tiled=True),
        lax.all_to_all(adjoint_done, "mp", split_axis=1, concat_axis=0, tiled=True),
    )
    summed_in, summed_out = (
        lax.psum_scatter(acc_in, "dp", scatter_dimension=0, tiled=True),
        lax.psum_scatter(acc_out, "dp", scatter_dimension=1, tiled=True),
    )
    return (state, adjoint, step_size * summed_in, step_size * summed_out)


def solution(mesh):
    in_specs = (
        P("dp", "mp"),
        P("dp", "mp"),
        P(None, "dp", None),
        P(None, "mp"),
        P("mp"),
        P("mp", None),
        P(),
        P(),
    )
    out_specs = (P("dp", "mp"), P("dp", "mp"), P("dp", "mp"), P("mp", "dp"))
    return jax.shard_map(body, mesh=mesh, in_specs=in_specs, out_specs=out_specs, check_vma=False)
```

profile of v0, /device:TPU:0, one launch (start us, length us, event | category | flops | bytes accessed | tf_op | source)
XLA Modules:
  0.0 394.4 jit_solution(2079276398997118393)
XLA Ops:
  8.7 4.3 %all-to-all-start = ((f32[4,64,128]{2,1,0:T(8,128)}), f32[4,64,128]{2,1,0:T(8,128)S(1)}, u32[]{:S(2)}, u32[]{:S(2)}) async-start(f32[4,64,128]{2,1,0:T(8,128)} %bitcast.61), calls=%async_computation | async-start | bytes 262144 | tf_op jit(solution)/shard_map/all_to_all | solution.py:26
  13.6 5.3 %all-gather = bf16[4,1,512]{2,1,0:T(2,128)(2,1)S(1)} all-gather(bf16[1,1,512]{2,1,0:T(2,128)(2,1)S(1)} %reshape.26), channel_id=1, replica_groups=mesh['dp'=8,'mp'=4] {'mp'}, dimensions={0}, use_global_device_ids=true | all-gather | bytes 5120 | tf_op jit(solution)/shard_map/all_gather | solution.py:32
  19.0 3.3 all-to-all-start.1
  22.4 6.4 %all-to-all-done.1 = f32[4,64,128]{2,1,0:T(8,128)S(1)} async-done(((f32[4,64,128]{2,1,0:T(8,128)}), f32[4,64,128]{2,1,0:T(8,128)S(1)}, u32[]{:S(2)}, u32[]{:S(2)}) %all-to-all-start.1) | async-done | bytes 131104 | tf_op jit(solution)/shard_map/all_to_all | solution.py:27
  28.8 7.5 %all-gather.4.cloned.1.call-done = bf16[512,2048]{1,0:T(8,128)(2,1)} async-done(((bf16[512,512]{1,0:T(8,128)(2,1)}), bf16[512,2048]{1,0:T(8,128)(2,1)}) %all-gather.4.cloned.1.call-update) | async-done | bytes 2097168 | tf_op jit(solution)/shard_map/all_gather | solution.py:30
  36.3 24.2 %all-gather.6.cloned.1.call-done = bf16[2048,512]{1,0:T(8,128)(2,1)} async-done(((bf16[512,512]{1,0:T(8,128)(2,1)}), bf16[2048,512]{1,0:T(8,128)(2,1)}) %all-gather.6.cloned.1.call-update) | async-done | bytes 2097168 | tf_op jit(solution)/shard_map/all_gather | solution.py:31
  60.4 93.5 %while.22 = (s32[]{:T(128)}, f32[64,512]{1,0:T(8,128)S(1)}, f32[64,512]{1,0:T(8,128)S(1)}, f32[512,2048]{0,1:T(8,128)}, f32[2048,512]{1,0:T(8,128)}, /*index=5*/...) while((s32[]{:T(128)}, f32[64,512]{1,0:T(8,128)S(1)}, ...), condition=%wide.region_1.2_spmd.clone, body=%wide.region_0.1_spmd.clone.sunk | while | flops 810811392 | bytes 113078696 | solution.py:57
  74.4 2.3 fusion.52
  86.0 2.3 fusion.52
  97.7 2.3 fusion.52
  109.4 2.3 fusion.52
  121.1 2.3 fusion.52
  132.8 2.3 fusion.52
  144.5 2.3 fusion.52
  153.9 5.4 %copy.27 = f32[2048,512]{0,1:T(8,128)} copy(f32[2048,512]{1,0:T(8,128)} %get-tuple-element.274) | data formatting | bytes 8388608 | tf_op jit(solution)/shard_map/while | solution.py:57
  159.4 5.5 %copy.26 = f32[512,2048]{1,0:T(8,128)} copy(f32[512,2048]{0,1:T(8,128)} %get-tuple-element.273) | data formatting | bytes 8388608 | tf_op jit(solution)/shard_map/while | solution.py:57
  164.9 38.9 %reduce-scatter.9.cloned.1.call-done = f32[512,512]{0,1:T(8,128)} async-done(((f32[2048,512]{0,1:T(8,128)}), f32[512,512]{0,1:T(8,128)}) %reduce-scatter.9.cloned.1.call-update) | async-done | bytes 1048592 | tf_op jit(solution)/shard_map/reduce_scatter | solution.py:62
  204.0 46.8 %reduce-scatter.5.cloned.1.call-done = f32[512,512]{1,0:T(8,128)} async-done(((f32[512,2048]{1,0:T(8,128)}), f32[512,512]{1,0:T(8,128)}) %reduce-scatter.5.cloned.1.call-update) | async-done | bytes 1048592 | tf_op jit(solution)/shard_map/reduce_scatter | solution.py:61
  251.4 3.3 all-to-all-start.2
  255.4 3.9 all-to-all-done.2
  259.3 3.3 all-to-all-start.3
  262.7 4.6 %all-to-all-done.3 = f32[64,4,128]{2,0,1:T(8,128)S(1)} async-done(((f32[64,4,128]{2,0,1:T(8,128)}), f32[64,4,128]{2,0,1:T(8,128)S(1)}, u32[]{:S(2)}, u32[]{:S(2)}) %all-to-all-start.3) | async-done | bytes 131104 | tf_op jit(solution)/shard_map/all_to_all | solution.py:66
  267.2 50.9 %reduce-scatter.11.cloned.1.call-done = f32[512,64]{0,1:T(8,128)} async-done(((f32[512,512]{0,1:T(8,128)}), f32[512,64]{0,1:T(8,128)}) %reduce-scatter.11.cloned.1.call-update) | async-done | bytes 131088 | tf_op jit(solution)/shard_map/reduce_scatter | solution.py:70
  319.8 64.9 %reduce-scatter.7.cloned.1.call-done = f32[64,512]{1,0:T(8,128)} async-done(((f32[512,512]{1,0:T(8,128)}), f32[64,512]{1,0:T(8,128)}) %reduce-scatter.7.cloned.1.call-update) | async-done | bytes 131088 | tf_op jit(solution)/shard_map/reduce_scatter | solution.py:69
  (198 shorter events, 84.6 us)
Async XLA Ops:
  7.2 11.8 %copy-start = (bf16[8,256,512]{2,1,0:T(8,128)(2,1)S(1)}, bf16[8,256,512]{2,1,0:T(8,128)(2,1)}, u32[]{:S(2)}) copy-start(bf16[8,256,512]{2,1,0:T(8,128)(2,1)} %param.12) | copy-start | bytes 6291460
  7.2 29.1 %all-gather.4.cloned.1.call-start = ((), (), s32[]{:S(2)}) async-start(), calls=%async_computation.8 | async-start | bytes 2621440 | tf_op jit(solution)/shard_map/all_gather | solution.py:30
  7.9 52.5 %all-gather.6.cloned.1.call-start = ((), (), s32[]{:S(2)}) async-start(), calls=%async_computation.9 | async-start | bytes 2621440 | tf_op jit(solution)/shard_map/all_gather | solution.py:31
  8.7 10.3 %all-to-all-start = ((f32[4,64,128]{2,1,0:T(8,128)}), f32[4,64,128]{2,1,0:T(8,128)S(1)}, u32[]{:S(2)}, u32[]{:S(2)}) async-start(f32[4,64,128]{2,1,0:T(8,128)} %bitcast.61), calls=%async_computation | async-start | bytes 262144 | tf_op jit(solution)/shard_map/all_to_all | solution.py:26
  19.0 9.8 %all-to-all-start.1 = ((f32[4,64,128]{2,1,0:T(8,128)}), f32[4,64,128]{2,1,0:T(8,128)S(1)}, u32[]{:S(2)}, u32[]{:S(2)}) async-start(f32[4,64,128]{2,1,0:T(8,128)} %bitcast.62), calls=%async_computation.1 | async-start | bytes 262144 | tf_op jit(solution)/shard_map/all_to_all | solution.py:27
  22.3 181.6 %reduce-scatter.9.cloned.1.call-start = ((), (), s32[]{:S(2)}) async-start(), calls=%async_computation.12 | async-start | bytes 5242880 | tf_op jit(solution)/shard_map/reduce_scatter | solution.py:62
  60.4 4.6 %copy-start.5 = (f32[512,2048]{0,1:T(8,128)S(1)}, f32[512,2048]{0,1:T(8,128)}, u32[]{:S(2)}) copy-start(f32[512,2048]{0,1:T(8,128)} %get-tuple-element.418) | copy-start | bytes 12582916 | tf_op jit(solution)/shard_map/while
  72.1 4.6 %copy-start.5 = (f32[512,2048]{0,1:T(8,128)S(1)}, f32[512,2048]{0,1:T(8,128)}, u32[]{:S(2)}) copy-start(f32[512,2048]{0,1:T(8,128)} %get-tuple-element.418) | copy-start | bytes 12582916 | tf_op jit(solution)/shard_map/while
  76.7 3.5 copy-start.3
  83.8 4.6 %copy-start.5 = (f32[512,2048]{0,1:T(8,128)S(1)}, f32[512,2048]{0,1:T(8,128)}, u32[]{:S(2)}) copy-start(f32[512,2048]{0,1:T(8,128)} %get-tuple-element.418) | copy-start | bytes 12582916 | tf_op jit(solution)/shard_map/while
  95.5 4.6 %copy-start.5 = (f32[512,2048]{0,1:T(8,128)S(1)}, f32[512,2048]{0,1:T(8,128)}, u32[]{:S(2)}) copy-start(f32[512,2048]{0,1:T(8,128)} %get-tuple-element.418) | copy-start | bytes 12582916 | tf_op jit(solution)/shard_map/while
  100.1 3.5 copy-start.3
  107.2 4.6 %copy-start.5 = (f32[512,2048]{0,1:T(8,128)S(1)}, f32[512,2048]{0,1:T(8,128)}, u32[]{:S(2)}) copy-start(f32[512,2048]{0,1:T(8,128)} %get-tuple-element.418) | copy-start | bytes 12582916 | tf_op jit(solution)/shard_map/while
  111.8 3.5 copy-start.3
  118.8 4.6 %copy-start.5 = (f32[512,2048]{0,1:T(8,128)S(1)}, f32[512,2048]{0,1:T(8,128)}, u32[]{:S(2)}) copy-start(f32[512,2048]{0,1:T(8,128)} %get-tuple-element.418) | copy-start | bytes 12582916 | tf_op jit(solution)/shard_map/while
  123.5 3.5 copy-start.3
  130.5 4.6 %copy-start.5 = (f32[512,2048]{0,1:T(8,128)S(1)}, f32[512,2048]{0,1:T(8,128)}, u32[]{:S(2)}) copy-start(f32[512,2048]{0,1:T(8,128)} %get-tuple-element.418) | copy-start | bytes 12582916 | tf_op jit(solution)/shard_map/while
  135.2 3.5 copy-start.3
  142.2 4.6 %copy-start.5 = (f32[512,2048]{0,1:T(8,128)S(1)}, f32[512,2048]{0,1:T(8,128)}, u32[]{:S(2)}) copy-start(f32[512,2048]{0,1:T(8,128)} %get-tuple-element.418) | copy-start | bytes 12582916 | tf_op jit(solution)/shard_map/while
  159.3 91.4 %reduce-scatter.5.cloned.1.call-start = ((), (), s32[]{:S(2)}) async-start(), calls=%async_computation.10 | async-start | bytes 5242880 | tf_op jit(solution)/shard_map/reduce_scatter | solution.py:61
  164.9 153.3 %reduce-scatter.11.cloned.1.call-start = ((), (), s32[]{:S(2)}) async-start(), calls=%async_computation.13 | async-start | bytes 1179648 | tf_op jit(solution)/shard_map/reduce_scatter | solution.py:70
  203.9 180.8 %reduce-scatter.7.cloned.1.call-start = ((), (), s32[]{:S(2)}) async-start(), calls=%async_computation.11 | async-start | bytes 1179648 | tf_op jit(solution)/shard_map/reduce_scatter | solution.py:69
  251.4 7.9 %all-to-all-start.2 = ((f32[64,4,128]{2,0,1:T(8,128)}), f32[64,4,128]{2,0,1:T(8,128)S(1)}, u32[]{:S(2)}, u32[]{:S(2)}) async-start(f32[64,4,128]{2,0,1:T(8,128)} %copy_bitcast_fusion.3), calls=%async_computation.2 | async-start | bytes 262144 | tf_op jit(solution)/shard_map/all_to_all | solution.py:65
  259.3 7.9 %all-to-all-start.3 = ((f32[64,4,128]{2,0,1:T(8,128)}), f32[64,4,128]{2,0,1:T(8,128)S(1)}, u32[]{:S(2)}, u32[]{:S(2)}) async-start(f32[64,4,128]{2,0,1:T(8,128)} %copy_bitcast_fusion.2), calls=%async_computation.3 | async-start | bytes 262144 | tf_op jit(solution)/shard_map/all_to_all | solution.py:66
  (51 other events, 102.3 us)
Sparse Core Ops, SparseCore 0:
  9.5 26.6 all-gather.3
  37.8 22.5 all-gather.5
  159.5 44.3 reduce-scatter.8
  206.3 44.4 reduce-scatter.4
  254.0 64.1 reduce-scatter.10
  321.4 63.1 reduce-scatter.6
where the time goes:
time: 396 us; the launch traced here: 394 us
  waiting for transfers between devices  250 us (63%)
  matrix products  66.1 us (17%)
  local copies, waits for them, and re-layouts  40.3 us (10%)
  starting transfers between devices  14.5 us (4%)
  between operations  14.2 us (4%)
  blocking collectives  5.27 us (1%)
    reduce_scatter x1, waiting for transfers between devices, body(): lax.psum_scatter(acc_in, 'dp', scatter_dimension=0, tiled=True)  64.9 us
    reduce_scatter x1, waiting for transfers between devices, body(): lax.psum_scatter(acc_out, 'dp', scatter_dimension=1, tiled=True)  50.9 us
    reduce_scatter x1, waiting for transfers between devices, body(): lax.psum_scatter(full_in, 'mp', scatter_dimension=1, tiled=True)  46.8 us
    reduce_scatter x1, waiting for transfers between devices, body(): lax.psum_scatter(full_out, 'mp', scatter_dimension=0, tiled=True)  38.9 us
    while x128, local copies, waits for them, and re-layouts  26.6 us
    all_gather x1, waiting for transfers between devices, body(): lax.all_gather(w_out, 'mp', axis=0, tiled=True)  24.2 us
    dot_general x8, matrix products, local_terms(): back = jnp.dot(a_low, w_out.T, preferred_element_type=jnp.float32)  18.8 us
    dot_general x8, matrix products, local_terms(): jnp.dot(z_low, w_in, preferred_element_type=jnp.float32) + b_in  17.8 us
  transfers between devices with their start and end apart: 10, of which 9 were waited for; matrix products, arithmetic and copies ran while one was open for 2% of the time, Pallas kernels for 0%

commit v1 on v0

v1 whole, which is shorter than its diff:
```python
import functools

import jax
import jax.numpy as jnp
from jax import lax
from jax.experimental import pallas as pl
from jax.experimental.pallas import tpu as pltpu
from jax.sharding import PartitionSpec as P

STEPS = 8
F32 = jnp.float32
LOW = jnp.bfloat16


def dot(x, y, cx, cy):
    return lax.dot_general(x, y, (((cx,), (cy,)), ((), ())), preferred_element_type=F32)


def kernel(
    mp, dp, state, adjoint, incr, w_in, b_in, w_out, b_out, sigma,
    state_o, adjoint_o, gin_o, gout_o,
    wi, wo, bi, rz, ra, noise, z_s, a_s, zall, aall, dall, hall,
    sz, sa, fz, fa, s1, r1, s2, r2, acc, s3, r3,
    sem_loc, sem_ws, sem_wf, sem_wr, sem_ss, sem_sr, sem_fs, sem_fr,
    sem_1s, sem_1r, sem_2s, sem_2r, sem_3s, sem_3r,
):
    step_size = 1.0 / STEPS
    m = lax.axis_index("mp")
    d = lax.axis_index("dp")
    ny = mp // 2
    y, c = m // 2, m % 2
    partner = y * 2 + (1 - c)
    rows = state.shape[0] // mp
    cols = state.shape[1]
    hs = w_in.shape[1]

    def remote(src, dst, ssem, rsem, axis, who):
        return pltpu.make_async_remote_copy(
            src_ref=src, dst_ref=dst, send_sem=ssem, recv_sem=rsem,
            device_id={axis: who}, device_id_type=pl.DeviceIdType.MESH)

    row0 = pl.multiple_of(m * rows, rows)
    loc = [
        pltpu.make_async_copy(incr.at[:, pl.ds(row0, rows), :], noise, sem_loc.at[0]),
        pltpu.make_async_copy(w_in, wi.at[m], sem_loc.at[1]),
        pltpu.make_async_copy(w_out, wo.at[m], sem_loc.at[2]),
    ]
    for q in loc:
        q.start()

    bar = pltpu.get_barrier_semaphore()
    for k in range(1, mp):
        pl.semaphore_signal(bar, inc=1, device_id={"mp": (m + k) % mp},
                            device_id_type=pl.DeviceIdType.MESH)
    for k in range(1, dp):
        pl.semaphore_signal(bar, inc=1, device_id={"dp": (d + k) % dp},
                            device_id_type=pl.DeviceIdType.MESH)
    pl.semaphore_wait(bar, mp - 1 + dp - 1)

    sends = []
    for k in range(1, mp):
        p = (m + k) % mp
        prow = pl.ds(pl.multiple_of(p * rows, rows), rows)
        for i, (src, dst) in enumerate(((state, rz), (adjoint, ra))):
            q = remote(src.at[prow, :], dst.at[m], sem_ss.at[i, k], sem_sr.at[i, m], "mp", p)
            q.start()
            sends.append(q)
    whole = ((b_in, bi), (w_in, wi), (w_out, wo))
    for k in range(1, ny):
        p = ((y + k) % ny) * 2 + c
        for i, (src, dst) in enumerate(whole):
            q = remote(src, dst.at[m], sem_ws.at[i, k], sem_wr.at[i, m], "mp", p)
            q.start()
            sends.append(q)
    for i, (src, dst) in enumerate(whole):
        q = remote(src, dst.at[m], sem_ws.at[i, 0], sem_wr.at[i, m], "mp", partner)
        q.start()
        sends.append(q)
    rz[m] = state[pl.ds(row0, rows), :]
    ra[m] = adjoint[pl.ds(row0, rows), :]
    bi[m] = b_in[...]
    for k in range(1, ny):
        slot = ((y + k) % ny) * 2 + c
        for i, (src, dst) in enumerate(whole):
            remote(src, dst.at[slot], sem_wf.at[i, k], sem_wr.at[i, slot], "mp", partner).wait_recv()
            q = remote(dst.at[slot], dst.at[slot], sem_wf.at[i, k], sem_wr.at[i, slot], "mp", partner)
            q.start()
            sends.append(q)
    for k in range(1, mp):
        p = (m + k) % mp
        for i, dst in enumerate((rz, ra)):
            remote(dst.at[p], dst.at[p], sem_ss.at[i, k], sem_sr.at[i, p], "mp", p).wait_recv()
    for q in loc:
        q.wait()
    z_s[...] = jnp.concatenate([rz[p] for p in range(mp)], axis=1)
    a_s[...] = jnp.concatenate([ra[p] for p in range(mp)], axis=1)
    for k in range(ny):
        slot = ((y + k) % ny) * 2 + (1 - c)
        for i, (src, dst) in enumerate(whole):
            remote(src, dst.at[slot], sem_ws.at[i, 0], sem_wr.at[i, slot], "mp", partner).wait_recv()
    for q in sends:
        q.wait_send()

    def advance(counter, carry):
        level = STEPS - 1 - counter
        at = pl.ds(pl.multiple_of(counter * rows, rows), rows)
        z, a = z_s[...], a_s[...]
        z_low, a_low = z.astype(LOW), a.astype(LOW)
        zall[at, :] = z_low
        aall[at, :] = a_low
        drift = b_out[...]
        pull = None
        for s in range(mp):
            hidden = jnp.tanh(dot(z_low, wi[s], 1, 0) + bi[s])
            back = dot(a_low, wo[s], 1, 1)
            hidden_low = hidden.astype(LOW)
            delta = (back * (1.0 - hidden * hidden)).astype(LOW)
            hall[s, at, :] = hidden_low
            dall[s, at, :] = delta
            drift = drift + dot(hidden_low, wo[s], 1, 0)
            part = dot(delta, wi[s], 1, 1)
            pull = part if pull is None else pull + part
        a_s[...] = a + step_size * pull
        z_s[...] = z - step_size * drift - sigma[...] * noise[level].astype(F32)
        return carry

    lax.fori_loop(0, STEPS, advance, 0)

    for p in range(mp):
        sz[p] = z_s[:, p * cols:(p + 1) * cols]
        sa[p] = a_s[:, p * cols:(p + 1) * cols]

    terms = ((zall, dall), (aall, hall))

    def term(i, s):
        x, v = terms[i]
        return dot(x[...], v[s], 0, 0)

    sends = []

    def to_partner(i, k):
        s = ((y + k) % ny) * 2 + (1 - c)
        s1[k, i] = term(i, s).astype(LOW)
        q = remote(s1.at[k, i], r1.at[k, i], sem_1s.at[k, i], sem_1r.at[k, i], "mp", partner)
        q.start()
        sends.append(q)

    def from_partner(i, k):
        remote(s1.at[k, i], r1.at[k, i], sem_1s.at[k, i], sem_1r.at[k, i], "mp", partner).wait_recv()

    for i in range(2):
        for k in range(1, ny):
            to_partner(i, k)
    for k in range(1, mp):
        p = (m + k) % mp
        for i, (src, dst) in enumerate(((sz, fz), (sa, fa))):
            q = remote(src.at[p], dst.at[m], sem_fs.at[i, k], sem_fr.at[i, m], "mp", p)
            q.start()
            sends.append(q)
    for i in range(2):
        for k in range(1, ny):
            own = term(i, ((y + k) % ny) * 2 + c)
            from_partner(i, k)
            s2[k, i] = (own + r1[k, i].astype(F32)).astype(LOW)
            q = remote(s2.at[k, i], r2.at[k, i], sem_2s.at[k, i], sem_2r.at[k, i],
                       "mp", ((y + k) % ny) * 2 + c)
            q.start()
            sends.append(q)
    for i in range(2):
        to_partner(i, 0)
    for i in range(2):
        acc[i] = term(i, m)
    for i in range(2):
        from_partner(i, 0)
        acc[i] = acc[i] + r1[0, i].astype(F32)
    state_o[pl.ds(row0, rows), :] = sz[m]
    adjoint_o[pl.ds(row0, rows), :] = sa[m]
    for k in range(1, mp):
        p = (m + k) % mp
        for i, (dst, out) in enumerate(((fz, state_o), (fa, adjoint_o))):
            remote(dst.at[p], dst.at[p], sem_fs.at[i, k], sem_fr.at[i, p], "mp", p).wait_recv()
            out[pl.ds(pl.multiple_of(p * rows, rows), rows), :] = dst[p]
    drows = acc.shape[1] // dp
    for i in range(2):
        for k in range(1, ny):
            remote(s2.at[k, i], r2.at[k, i], sem_2s.at[k, i], sem_2r.at[k, i], "mp", partner).wait_recv()
            acc[i] = acc[i] + r2[k, i].astype(F32)
        s3[i] = acc[i].astype(LOW).reshape(dp, drows, hs)
        for k in range(1, dp):
            p = (d + k) % dp
            q = remote(s3.at[i, p], r3.at[i, d], sem_3s.at[i, k], sem_3r.at[i, d], "dp", p)
            q.start()
            sends.append(q)
    for i in range(2):
        total = acc[i, pl.ds(pl.multiple_of(d * drows, drows), drows), :]
        for k in range(1, dp):
            p = (d + k) % dp
            remote(s3.at[i, p], r3.at[i, p], sem_3s.at[i, k], sem_3r.at[i, p], "dp", p).wait_recv()
            total = total + r3[i, p].astype(F32)
        total = total * step_size
        if i == 0:
            gin_o[...] = total
        else:
            gout_o[...] = total.T
    for q in sends:
        q.wait_send()


def body(mp, dp, state_end, adjoint_end, increments, w_in, b_in, w_out, b_out, sigma):
    br, cols = state_end.shape
    rows = br // mp
    width, hs = w_in.shape
    steps = increments.shape[0]
    ny = mp // 2
    drows = width // dp
    vm = pl.BlockSpec(memory_space=pltpu.VMEM)
    dma = pltpu.SemaphoreType.DMA
    scratch = [
        pltpu.VMEM((mp, width, hs), LOW),
        pltpu.VMEM((mp, hs, width), LOW),
        pltpu.VMEM((mp, 1, hs), F32),
        pltpu.VMEM((mp, rows, cols), F32),
        pltpu.VMEM((mp, rows, cols), F32),
        pltpu.VMEM((steps, rows, width), LOW),
        pltpu.VMEM((rows, width), F32),
        pltpu.VMEM((rows, width), F32),
        pltpu.VMEM((steps * rows, width), LOW),
        pltpu.VMEM((steps * rows, width), LOW),
        pltpu.VMEM((mp, steps * rows, hs), LOW),
        pltpu.VMEM((mp, steps * rows, hs), LOW),
        pltpu.VMEM((mp, rows, cols), F32),
        pltpu.VMEM((mp, rows, cols), F32),
        pltpu.VMEM((mp, rows, cols), F32),
        pltpu.VMEM((mp, rows, cols), F32),
        pltpu.VMEM((ny, 2, width, hs), LOW),
        pltpu.VMEM((ny, 2, width, hs), LOW),
        pltpu.VMEM((ny, 2, width, hs), LOW),
        pltpu.VMEM((ny, 2, width, hs), LOW),
        pltpu.VMEM((2, width, hs), F32),
        pltpu.VMEM((2, dp, drows, hs), LOW),
        pltpu.VMEM((2, dp, drows, hs), LOW),
        dma((3,)), dma((3, ny)), dma((3, ny)), dma((3, mp)),
        dma((2, mp)), dma((2, mp)), dma((2, mp)), dma((2, mp)),
        dma((ny, 2)), dma((ny, 2)), dma((ny, 2)), dma((ny, 2)),
        dma((2, dp)), dma((2, dp)),
    ]
    return pl.pallas_call(
        functools.partial(kernel, mp, dp),
        out_shape=(
            jax.ShapeDtypeStruct((br, cols), F32),
            jax.ShapeDtypeStruct((br, cols), F32),
            jax.ShapeDtypeStruct((drows, hs), F32),
            jax.ShapeDtypeStruct((hs, drows), F32),
        ),
        in_specs=[vm, vm, pl.BlockSpec(memory_space=pl.ANY), vm, vm, vm, vm, vm],
        out_specs=(vm, vm, vm, vm),
        scratch_shapes=scratch,
        compiler_params=pltpu.CompilerParams(
            collective_id=0, has_side_effects=True, vmem_limit_bytes=56 * 1024 * 1024),
    )(state_end, adjoint_end, increments, w_in, b_in.reshape(1, -1), w_out,
      b_out.reshape(1, -1), sigma.reshape(1, -1))


def solution(mesh):
    mp, dp = mesh.shape["mp"], mesh.shape["dp"]
    in_specs = (
        P("dp", "mp"),
        P("dp", "mp"),
        P(None, "dp", None),
        P(None, "mp"),
        P("mp"),
        P("mp", None),
        P(),
        P(),
    )
    out_specs = (P("dp", "mp"), P("dp", "mp"), P("dp", "mp"), P("mp", "dp"))
    return jax.shard_map(functools.partial(body, mp, dp), mesh=mesh, in_specs=in_specs,
                         out_specs=out_specs, check_vma=False)
```

time: 396 us -> 101 us (0.26)
  waiting for transfers between devices: 250 us -> 0 us
  Pallas kernels: 0 us -> 93.2 us
  matrix products: 66.1 us -> 0 us
  local copies, waits for them, and re-layouts: 40.3 us -> 6.42 us
  starting transfers between devices: 14.5 us -> 0 us
  between operations: 14.2 us -> 0.64 us
  blocking collectives: 5.27 us -> 0 us
    reduce_scatter x4 -> x0, waiting for transfers between devices: 202 us -> none  [the longest x1 64.9 us: body(): lax.psum_scatter(acc_in, 'dp', scatter_dimension=0, tiled=True)]
    pallas_call x0 -> x1, Pallas kernels: none -> 93.2 us  [body(): pl.pallas_call(functools.partial(kernel, mp, dp), out_shape=(jax.ShapeDty...]
    dot_general x48 -> x0, matrix products: 66.1 us -> none  [the longest x8 18.8 us: local_terms(): back = jnp.dot(a_low, w_out.T, preferred_element_type=jnp.float32)]
    while x130 -> x0, local copies, waits for them, and re-layouts: 37.5 us -> none
    all_gather x2 -> x0, waiting for transfers between devices: 31.6 us -> none  [the longest x1 24.2 us: body(): lax.all_gather(w_out, 'mp', axis=0, tiled=True)]
    all_to_all x4 -> x0, waiting for transfers between devices: 14.9 us -> none  [the longest x1 6.39 us: body(): lax.all_to_all(adjoint_end, 'mp', split_axis=0, concat_axis=1, tiled=True)]
    all_to_all x4 -> x0, starting transfers between devices: 14.3 us -> none  [the longest x1 4.28 us: body(): lax.all_to_all(state_end, 'mp', split_axis=0, concat_axis=1, tiled=True)]
    all_gather x1 -> x0, blocking collectives: 5.27 us -> none  [body(): lax.all_gather(b_in.astype(jnp.bfloat16), 'mp', axis=0, tiled=True)]
  transfers between devices with their start and end apart: 10 -> 0, of which waited for: 9 -> 0; matrix products, arithmetic and copies ran while one was open for 2% -> 0% of each run, Pallas kernels for 0% -> 0%
where the time goes in v1:
time: 101 us; the launch traced here: 100 us
  Pallas kernels  93.2 us (92%)
  local copies, waits for them, and re-layouts  6.42 us (6%)
    pallas_call x1, Pallas kernels, body(): pl.pallas_call(functools.partial(kernel, mp, dp), out_shape=(jax.ShapeDty...  93.2 us
    unnamed x3, local copies, waits for them, and re-layouts  4.7 us

profile of v1, /device:TPU:0, one launch (start us, length us, event | category | flops | bytes accessed | tf_op | source)
XLA Modules:
  0.0 100.2 jit_solution(3109047156964962269)
XLA Ops:
  0.6 93.2 %shard_map.111 = (f32[256,128]{1,0:T(8,128)}, f32[256,128]{1,0:T(8,128)}, f32[64,512]{1,0:T(8,128)}, f32[512,64]{1,0:T(8,128)}) custom-call(f32[256,128]{1,0:T(8,128)} %state.1, f32[256,128]{1,0:T(8,128)} %adjoint.1, bf16[8,256,512]{2,1,0:T(8,128)(2,1)} %incr.1, bf16[512,512]{1,0:T(8,128)(2,1)} %w_in.1, f32[1,512]{1,0:T(1,128)} %bitcast.3, ...), custom_call_target="tpu_custom_call" | custom-call | tf_op jit(solution)/shard_map/pallas_call | solution.py:247
  93.8 1.7 %copy.12 = f32[512,64]{0,1:T(8,128)} copy(f32[512,64]{1,0:T(8,128)} %get-tuple-element.7) | data formatting | bytes 262144 | tf_op jit(solution)/shard_map/pallas_call | solution.py:247
  95.5 1.6 %copy.16 = f32[256,128]{1,0:T(8,128)} copy(f32[256,128]{1,0:T(8,128)} %get-tuple-element.12) | data formatting | bytes 262144
  97.1 1.6 %copy.17 = f32[256,128]{1,0:T(8,128)} copy(f32[256,128]{1,0:T(8,128)} %get-tuple-element.13) | data formatting | bytes 262144
  98.7 1.6 %copy.18 = f32[64,512]{1,0:T(8,128)} copy(f32[64,512]{1,0:T(8,128)} %get-tuple-element.14) | data formatting | bytes 262144

commit v2 on v1

v2 whole, which is shorter than its diff:
```python
import functools

import jax
import jax.numpy as jnp
from jax import lax
from jax.experimental import pallas as pl
from jax.experimental.pallas import tpu as pltpu
from jax.sharding import PartitionSpec as P

STEPS = 8
CUTS = 2
COLS = 2
F32 = jnp.float32
LOW = jnp.bfloat16


def dot(x, y, cx, cy):
    return lax.dot_general(x, y, (((cx,), (cy,)), ((), ())), preferred_element_type=F32)


def kernel(
    mp, dp, state, adjoint, incr, w_in, b_in, w_out, b_out, sigma,
    state_o, adjoint_o, gin_o, gout_o,
    wi, wo, bi, rz, ra, noise, z_s, a_s, zall, aall, dall, hall,
    sz, sa, fz, fa, s1, r1, s2a, r2a, s2b, r2b, sxa, rxa, sxb, rxb, kb, half, acc, za, s3, r3,
    sem_loc, sem_ys, sem_xs, sem_ps, sem_ws, sem_wr, sem_bs, sem_br, sem_ss, sem_sr, sem_fs, sem_fr,
    sem_1s, sem_1r, sem_2s, sem_2r, sem_as, sem_ar, sem_cs, sem_cr, sem_3s, sem_3r,
):
    step_size = 1.0 / STEPS
    m = lax.axis_index("mp")
    d = lax.axis_index("dp")
    ny = mp // 2
    y, c = m // 2, m % 2
    partner = y * 2 + (1 - c)
    rows = state.shape[0] // mp
    cols = state.shape[1]
    hs = w_in.shape[1]

    def remote(src, dst, ssem, rsem, axis, who):
        return pltpu.make_async_remote_copy(
            src_ref=src, dst_ref=dst, send_sem=ssem, recv_sem=rsem,
            device_id={axis: who}, device_id_type=pl.DeviceIdType.MESH)

    row0 = pl.multiple_of(m * rows, rows)
    loc = [
        pltpu.make_async_copy(incr.at[:, pl.ds(row0, rows), :], noise, sem_loc.at[0]),
        pltpu.make_async_copy(w_in, wi.at[m], sem_loc.at[1]),
        pltpu.make_async_copy(w_out, wo.at[m], sem_loc.at[2]),
    ]
    for q in loc:
        q.start()

    bar = pltpu.get_barrier_semaphore()
    for k in range(1, mp):
        pl.semaphore_signal(bar, inc=1, device_id={"mp": (m + k) % mp},
                            device_id_type=pl.DeviceIdType.MESH)
    for k in range(1, dp):
        pl.semaphore_signal(bar, inc=1, device_id={"dp": (d + k) % dp},
                            device_id_type=pl.DeviceIdType.MESH)
    pl.semaphore_wait(bar, mp - 1 + dp - 1)

    sends = []

    def go(*args):
        q = remote(*args)
        q.start()
        sends.append(q)

    def share(p, k):
        prow = pl.ds(pl.multiple_of(p * rows, rows), rows)
        for i, (src, dst) in enumerate(((state, rz), (adjoint, ra))):
            go(src.at[prow, :], dst.at[m], sem_ss.at[i, k], sem_sr.at[i, m], "mp", p)

    h = d % 2
    beside = d + 1 - 2 * h
    weights = ((w_in, wi), (w_out, wo))
    span = w_in.shape[0] // (2 * CUTS)

    def piece(q):
        return pl.ds(pl.multiple_of(q * span, span), span)

    for j in range(CUTS):
        q = h * CUTS + j
        for i, (src, dst) in enumerate(weights):
            for k in range(1, ny):
                go(src.at[piece(q), :], dst.at[m, piece(q), :], sem_ys.at[i, k, j],
                   sem_wr.at[i, m, q], "mp", ((y + k) % ny) * 2 + c)
    share(partner, 0)
    for i, (src, dst) in enumerate(weights):
        go(src, dst.at[m], sem_ws.at[i], sem_wr.at[i, m, 0], "mp", partner)
    for k in range(1, mp):
        go(b_in, bi.at[m], sem_bs.at[k], sem_br.at[m], "mp", (m + k) % mp)
    for k in range(1, ny):
        for e in range(2):
            share(((y + k) % ny) * 2 + e, 2 * k + e)
    rz[m] = state[pl.ds(row0, rows), :]
    ra[m] = adjoint[pl.ds(row0, rows), :]
    bi[m] = b_in[...]

    def arrived(i, slot, q):
        dst = weights[i][1]
        ref = dst.at[slot, piece(q), :]
        remote(ref, ref, sem_ys.at[0, 0, 0], sem_wr.at[i, slot, q], "mp", partner).wait_recv()
        return ref

    def hand_on(i, k, half, j):
        slot = ((y + k) % ny) * 2 + c
        q = (h if half == 0 else 1 - h) * CUTS + j
        ref = arrived(i, slot, q)
        if half == 0:
            go(ref, ref, sem_xs.at[i, k, j], sem_wr.at[i, slot, q], "dp", beside)
        go(ref, ref, sem_ps.at[i, k, half * CUTS + j], sem_wr.at[i, slot, q], "mp", partner)

    order = [(i, j) for j in range(CUTS) for i in range(2)]
    for n in range(len(order) + 2):
        for k in range(1, ny):
            if n < len(order):
                hand_on(order[n][0], k, 0, order[n][1])
            if n >= 2:
                hand_on(order[n - 2][0], k, 1, order[n - 2][1])
    for k in range(1, mp):
        p = (m + k) % mp
        remote(b_in, bi.at[p], sem_bs.at[k], sem_br.at[p], "mp", p).wait_recv()
        for i, dst in enumerate((rz, ra)):
            remote(dst.at[p], dst.at[p], sem_ss.at[i, k], sem_sr.at[i, p], "mp", p).wait_recv()
    for q in loc:
        q.wait()
    z_s[...] = jnp.concatenate([rz[p] for p in range(mp)], axis=1)
    a_s[...] = jnp.concatenate([ra[p] for p in range(mp)], axis=1)
    for i, (src, dst) in enumerate(weights):
        remote(src, dst.at[partner], sem_ws.at[i], sem_wr.at[i, partner, 0], "mp", partner).wait_recv()
    for k in range(1, ny):
        for i in range(2):
            for q in range(2 * CUTS):
                arrived(i, ((y + k) % ny) * 2 + (1 - c), q)
    for q in sends:
        q.wait_send()

    def advance(counter, carry):
        level = STEPS - 1 - counter
        at = pl.ds(pl.multiple_of(counter * rows, rows), rows)
        z, a = z_s[...], a_s[...]
        z_low, a_low = z.astype(LOW), a.astype(LOW)
        zall[at, :] = z_low
        aall[at, :] = a_low
        drift = b_out[...]
        pull = None
        for s in range(mp):
            hidden = jnp.tanh(dot(z_low, wi[s], 1, 0) + bi[s])
            back = dot(a_low, wo[s], 1, 1)
            hidden_low = hidden.astype(LOW)
            delta = (back * (1.0 - hidden * hidden)).astype(LOW)
            hall[s, at, :] = hidden_low
            dall[s, at, :] = delta
            drift = drift + dot(hidden_low, wo[s], 1, 0)
            part = dot(delta, wi[s], 1, 1)
            pull = part if pull is None else pull + part
        a_s[...] = a + step_size * pull
        z_s[...] = z - step_size * drift - sigma[...] * noise[level].astype(F32)
        return carry

    lax.fori_loop(0, STEPS, advance, 0)

    for p in range(mp):
        sz[p] = z_s[:, p * cols:(p + 1) * cols]
        sa[p] = a_s[:, p * cols:(p + 1) * cols]

    terms = ((zall, dall), (aall, hall))
    dpq, cw = dp // 2, hs // COLS
    drows = w_in.shape[0] // dp
    quad = d // 2
    sends.clear()

    def over_y(k):
        return ((y + k) % ny) * 2 + c

    def landed(ref, sem):
        remote(ref, ref, sem_ys.at[0, 0, 0], sem, "mp", partner).wait_recv()
        return ref[...].astype(F32)

    def term(i, s, j):
        x, v = terms[i]
        return dot(x[...], v[s, :, j * cw:(j + 1) * cw], 0, 0)

    def to_partner(i, j, k):
        s1[i, j, k] = term(i, ((y + k) % ny) * 2 + (1 - c), j).astype(LOW)
        go(s1.at[i, j, k], r1.at[i, j, k], sem_1s.at[i, j, k], sem_1r.at[i, j, k], "mp", partner)

    def paired(i, j, k):
        own = term(i, over_y(k), j)
        return own + landed(r1.at[i, j, k], sem_1r.at[i, j, k])

    def split(value):
        half[...] = value.reshape(dpq, 2, drows, cw)
        return half[:, h], half[:, 1 - h]

    def first_y(j):
        for k in range(1, ny):
            s2a[j, k] = paired(0, j, k).astype(LOW)
            go(s2a.at[j, k], r2a.at[j, k], sem_2s.at[0, j, k], sem_2r.at[0, j, k], "mp", over_y(k))

    def first_x(j):
        value = acc[j]
        for k in range(1, ny):
            value = value + landed(r2a.at[j, k], sem_2r.at[0, j, k])
        keep, give = split(value)
        za[0, j] = keep
        sxa[j] = give.astype(LOW)
        go(sxa.at[j], rxa.at[j], sem_as.at[j], sem_ar.at[j], "dp", beside)

    def second_x(j):
        for k in range(ny):
            keep, give = split(paired(1, j, k))
            kb[j, k] = keep
            sxb[j, k] = give.astype(LOW)
            go(sxb.at[j, k], rxb.at[j, k], sem_cs.at[j, k], sem_cr.at[j, k], "dp", beside)

    def second_y(j):
        for k in list(range(1, ny)) + [0]:
            value = kb[j, k] + landed(rxb.at[j, k], sem_cr.at[j, k])
            if k == 0:
                za[1, j] = value
            else:
                s2b[j, k] = value.astype(LOW)
                go(s2b.at[j, k], r2b.at[j, k], sem_2s.at[1, j, k], sem_2r.at[1, j, k],
                   "mp", over_y(k))

    def last(i, j):
        value = za[i, j]
        if i == 0:
            value = value + landed(rxa.at[j], sem_ar.at[j])
        else:
            for k in range(1, ny):
                value = value + landed(r2b.at[j, k], sem_2r.at[1, j, k])
        za[i, j] = value
        s3[i, j] = value.astype(LOW)
        for k in range(1, dpq):
            p = (quad + k) % dpq
            go(s3.at[i, j, p], r3.at[i, j, quad], sem_3s.at[i, j, k], sem_3r.at[i, j, quad],
               "dp", p * 2 + h)

    for j in range(COLS):
        for k in range(1, ny):
            to_partner(0, j, k)
        for k in range(ny):
            to_partner(1, j, k)
        first_y(j)
        second_x(j)
    for j in range(COLS):
        to_partner(0, j, 0)
    for j in range(COLS):
        acc[j] = paired(0, j, 0)
    for j in range(COLS):
        first_x(j)
        second_y(j)
    for k in range(1, mp):
        p = (m + k) % mp
        for i, (src, dst) in enumerate(((sz, fz), (sa, fa))):
            go(src.at[p], dst.at[m], sem_fs.at[i, k], sem_fr.at[i, m], "mp", p)
    for j in range(COLS):
        for i in range(2):
            last(i, j)
    state_o[pl.ds(row0, rows), :] = sz[m]
    adjoint_o[pl.ds(row0, rows), :] = sa[m]
    for k in range(1, mp):
        p = (m + k) % mp
        for i, (dst, out) in enumerate(((fz, state_o), (fa, adjoint_o))):
            out[pl.ds(pl.multiple_of(p * rows, rows), rows), :] = landed(dst.at[p], sem_fr.at[i, p])
    for j in range(COLS):
        for i, out in enumerate((gin_o, gout_o)):
            total = za[i, j, quad]
            for k in range(1, dpq):
                p = (quad + k) % dpq
                total = total + landed(r3.at[i, j, p], sem_3r.at[i, j, p])
            out[:, j * cw:(j + 1) * cw] = total * step_size
    for q in sends:
        q.wait_send()


def place(*refs):
    for src, dst in zip(refs[:4], refs[4:]):
        dst[...] = src[...]


def body(mp, dp, state_end, adjoint_end, increments, w_in, b_in, w_out, b_out, sigma):
    br, cols = state_end.shape
    rows = br // mp
    width, hs = w_in.shape
    steps = increments.shape[0]
    ny = mp // 2
    drows = width // dp
    dpq, cw = dp // 2, hs // COLS
    vm = pl.BlockSpec(memory_space=pltpu.VMEM)
    dma = pltpu.SemaphoreType.DMA
    scratch = [
        pltpu.VMEM((mp, width, hs), LOW),
        pltpu.VMEM((mp, hs, width), LOW),
        pltpu.VMEM((mp, 1, hs), F32),
        pltpu.VMEM((mp, rows, cols), F32),
        pltpu.VMEM((mp, rows, cols), F32),
        pltpu.VMEM((steps, rows, width), LOW),
        pltpu.VMEM((rows, width), F32),
        pltpu.VMEM((rows, width), F32),
        pltpu.VMEM((steps * rows, width), LOW),
        pltpu.VMEM((steps * rows, width), LOW),
        pltpu.VMEM((mp, steps * rows, hs), LOW),
        pltpu.VMEM((mp, steps * rows, hs), LOW),
        pltpu.VMEM((mp, rows, cols), F32),
        pltpu.VMEM((mp, rows, cols), F32),
        pltpu.VMEM((mp, rows, cols), F32),
        pltpu.VMEM((mp, rows, cols), F32),
        pltpu.VMEM((2, COLS, ny, width, cw), LOW),
        pltpu.VMEM((2, COLS, ny, width, cw), LOW),
        pltpu.VMEM((COLS, ny, width, cw), LOW),
        pltpu.VMEM((COLS, ny, width, cw), LOW),
        pltpu.VMEM((COLS, ny, dpq, drows, cw), LOW),
        pltpu.VMEM((COLS, ny, dpq, drows, cw), LOW),
        pltpu.VMEM((COLS, dpq, drows, cw), LOW),
        pltpu.VMEM((COLS, dpq, drows, cw), LOW),
        pltpu.VMEM((COLS, ny, dpq, drows, cw), LOW),
        pltpu.VMEM((COLS, ny, dpq, drows, cw), LOW),
        pltpu.VMEM((COLS, ny, dpq, drows, cw), F32),
        pltpu.VMEM((dpq, 2, drows, cw), F32),
        pltpu.VMEM((COLS, width, cw), F32),
        pltpu.VMEM((2, COLS, dpq, drows, cw), F32),
        pltpu.VMEM((2, COLS, dpq, drows, cw), LOW),
        pltpu.VMEM((2, COLS, dpq, drows, cw), LOW),
        dma((3,)), dma((2, ny, CUTS)), dma((2, ny, CUTS)), dma((2, ny, 2 * CUTS)),
        dma((2,)), dma((2, mp, 2 * CUTS)), dma((mp,)), dma((mp,)),
        dma((2, mp)), dma((2, mp)), dma((2, mp)), dma((2, mp)),
        dma((2, COLS, ny)), dma((2, COLS, ny)), dma((2, COLS, ny)), dma((2, COLS, ny)),
        dma((COLS,)), dma((COLS,)), dma((COLS, ny)), dma((COLS, ny)),
        dma((2, COLS, dpq)), dma((2, COLS, dpq)),
    ]
    outs = pl.pallas_call(
        functools.partial(kernel, mp, dp),
        out_shape=(
            jax.ShapeDtypeStruct((br, cols), F32),
            jax.ShapeDtypeStruct((br, cols), F32),
            jax.ShapeDtypeStruct((drows, hs), F32),
            jax.ShapeDtypeStruct((drows, hs), F32),
        ),
        in_specs=[vm, vm, pl.BlockSpec(memory_space=pl.ANY), vm, vm, vm, vm, vm],
        out_specs=(vm, vm, vm, vm),
        scratch_shapes=scratch,
        compiler_params=pltpu.CompilerParams(
            collective_id=0, has_side_effects=True, vmem_limit_bytes=56 * 1024 * 1024),
    )(state_end, adjoint_end, increments, w_in, b_in.reshape(1, -1), w_out,
      b_out.reshape(1, -1), sigma.reshape(1, -1))
    state, adjoint, gin, gout = pl.pallas_call(
        place,
        out_shape=tuple(jax.ShapeDtypeStruct(o.shape, o.dtype) for o in outs),
        in_specs=[vm] * 4,
        out_specs=(vm,) * 4,
    )(*outs)
    return state, adjoint, gin, gout.T


def solution(mesh):
    mp, dp = mesh.shape["mp"], mesh.shape["dp"]
    in_specs = (
        P("dp", "mp"),
        P("dp", "mp"),
        P(None, "dp", None),
        P(None, "mp"),
        P("mp"),
        P("mp", None),
        P(),
        P(),
    )
    out_specs = (P("dp", "mp"), P("dp", "mp"), P("dp", "mp"), P("mp", "dp"))
    return jax.shard_map(functools.partial(body, mp, dp), mesh=mesh, in_specs=in_specs,
                         out_specs=out_specs, check_vma=False)
```

time: 101 us -> 79.7 us (0.79)
  Pallas kernels: 93.2 us -> 78.9 us
  local copies, waits for them, and re-layouts: 6.42 us -> 0 us
    pallas_call x1, Pallas kernels: 93.2 us -> 77 us  [body(): pl.pallas_call(functools.partial(kernel, mp, dp), out_shape=(jax.ShapeDty...]
    unnamed x3 -> x0, local copies, waits for them, and re-layouts: 4.7 us -> none
    pallas_call x0 -> x1, Pallas kernels: none -> 1.89 us  [body(): pl.pallas_call(place, out_shape=tuple((jax.ShapeDtypeStruct(o.shape, o.dt...]
    pallas_call x1 -> x0, local copies, waits for them, and re-layouts: 1.72 us -> none  [body(): pl.pallas_call(functools.partial(kernel, mp, dp), out_shape=(jax.ShapeDty...]
where the time goes in v2:
time: 79.7 us; the launch traced here: 79.5 us
  Pallas kernels  78.9 us (99%)
    pallas_call x1, Pallas kernels, body(): pl.pallas_call(functools.partial(kernel, mp, dp), out_shape=(jax.ShapeDty...  77 us
    pallas_call x1, Pallas kernels, body(): pl.pallas_call(place, out_shape=tuple((jax.ShapeDtypeStruct(o.shape, o.dt...  1.89 us

profile of v2, /device:TPU:0, one launch (start us, length us, event | category | flops | bytes accessed | tf_op | source)
XLA Modules:
  0.0 79.5 jit_solution(12872204366512694823)
XLA Ops:
  0.6 77.0 %shard_map.111 = (f32[256,128]{1,0:T(8,128)}, f32[256,128]{1,0:T(8,128)}, f32[64,512]{1,0:T(8,128)}, f32[64,512]{1,0:T(8,128)}) custom-call(f32[256,128]{1,0:T(8,128)} %state.1, f32[256,128]{1,0:T(8,128)} %adjoint.1, bf16[8,256,512]{2,1,0:T(8,128)(2,1)} %incr.1, bf16[512,512]{1,0:T(8,128)(2,1)} %w_in.1, f32[1,512]{1,0:T(1,128)} %bitcast.4, ...), custom_call_target="tpu_custom_call" | custom-call | tf_op jit(solution)/shard_map/pallas_call | solution.py:335
  77.7 1.9 %shard_map.112 = (f32[256,128]{1,0:T(8,128)}, f32[256,128]{1,0:T(8,128)}, f32[64,512]{1,0:T(8,128)}, f32[64,512]{1,0:T(8,128)}) custom-call(f32[256,128]{1,0:T(8,128)} %get-tuple-element.12.refs_0_, f32[256,128]{1,0:T(8,128)} %get-tuple-element.13.refs_1_, f32[64,512]{1,0:T(8,128)} %get-tuple-element.14.refs_2_, f32[64,512]{1,0:T(8,128)} %get-tuple-element.15.refs_3_), custom_call_target="tpu_custom_call" | custom-call | tf_op jit(solution)/shard_map/pallas_call | solution.py:350
